TPU v7x, 32 devices: a whole 2x2x4 slice. The times are simulated.
32 devices in a mesh: section: 4 (over y, x), sc: 8 (over z, core).
Axes of the slice: x: 2, y: 2, z: 4, core: 2. Of those that a mesh axis runs over, the one named last changes fastest.
Arguments:
- observed_vector: float32 [1024, 14, 128], P('sc'), may hold values from -6 to 6
- propagation_matrix: float32 [1024, 8, 4, 128], P('sc', 'section'), may hold values from -0.5 to 0.5
- noise_var: float32 [1024], P('sc'), may hold values from 0.005 to 2.5, as said below
- sliced_constellation: int32 [1024, 14, 32], P('sc', None, 'section'), may hold values from 0 to 15
- detection_sequence: int32 [8], replicated, may hold values from 0 to 7, as said below
Outputs:
- estimates: float32 [1024, 14, 64], P('sc', None, 'section')
Inputs may be any that keep to these rules, and one draw needn't show every extreme that they name: `noise_var`: positive variances. `detection_sequence`: a permutation taken in blocks of 2 positions: each block of positions holds the 2 group ids 2 * m to 2 * m + 1 of one m, in a rotated order; the first block of positions takes m = 2, the second m = 0.
All inputs are finite; a program needn't handle non-finite values.
Results may differ from a plain program's by a relative error of at most 0.0001.
Values sent between devices are 32-bit elements; how exact they have to be, the bound alone decides.
A program may use at most 64 MiB of HBM per device.

v0:
```python
import jax
import jax.numpy as jnp
from jax import lax
from jax.sharding import PartitionSpec as P

ROOT_TEN = 3.1622776601683795


def padded_2(value, sides, width):
    for axis, dim in sides:
        size, length = (lax.axis_size(axis), value.shape[dim])
        up = [(i, (i + 1) % size) for i in range(size - 1)]
        down = [(j, i) for i, j in up]
        last = lax.slice_in_dim(value, length - width, length, axis=dim)
        leading = lax.slice_in_dim(value, 0, width, axis=dim)
        before = lax.ppermute(last, axis, up)
        after = lax.ppermute(leading, axis, down)
        value = jnp.concatenate([before, value, after], axis=dim)
    return value


def rotate(vectors):
    half = vectors.shape[-1] // 2
    return jnp.concatenate([-vectors[..., half:], vectors[..., :half]], axis=-1)


def symbol_values(constellation_labels):
    real_part = (2 * (constellation_labels % 4) - 3).astype(jnp.float32) / ROOT_TEN
    imag_part = (2 * (constellation_labels // 4) - 3).astype(jnp.float32) / ROOT_TEN
    return jnp.concatenate([real_part, imag_part], axis=-1)


def invert_small(gram):
    width = gram.shape[-1]
    entry = [[gram[..., i, j] for j in range(width)] for i in range(width)]
    lower = [[None] * width for i in range(width)]
    for j in range(width):
        pivot = entry[j][j]
        for k in range(j):
            pivot = pivot - lower[j][k] * lower[j][k]
        lower[j][j] = jnp.sqrt(pivot)
        recip = 1.0 / lower[j][j]
        for i in range(j + 1, width):
            value = entry[i][j]
            for k in range(j):
                value = value - lower[i][k] * lower[j][k]
            lower[i][j] = value * recip
    inv_lower = [[None] * width for i in range(width)]
    for i in range(width):
        inv_lower[i][i] = 1.0 / lower[i][i]
        for j in range(i):
            value = lower[i][j] * inv_lower[j][j]
            for k in range(j + 1, i):
                value = value + lower[i][k] * inv_lower[k][j]
            inv_lower[i][j] = -value * inv_lower[i][i]
    rows = []
    for i in range(width):
        cols = []
        for j in range(width):
            start = max(i, j)
            value = inv_lower[start][i] * inv_lower[start][j]
            for k in range(start + 1, width):
                value = value + inv_lower[k][i] * inv_lower[k][j]
            cols.append(value)
        rows.append(jnp.stack(cols, axis=-1))
    return jnp.stack(rows, axis=-2)


def filter_block(basis_all, noise):
    width = basis_all.shape[2]
    eye = jnp.eye(width, dtype=jnp.float32)
    gram = (
        jnp.einsum("sgik,sgjk->sgij", basis_all, basis_all, precision=lax.Precision.HIGHEST)
        + noise[:, None, None, None] * eye
    )
    inverse = invert_small(gram)
    filters = jnp.einsum("sgij,sgjk->sgik", inverse, basis_all, precision=lax.Precision.HIGHEST)
    diag = jnp.diagonal(inverse, axis1=2, axis2=3)[:, :, : width // 2]
    amplitude_level = 1.0 - noise[:, None, None] * diag
    return (filters, amplitude_level)


def local(observed_vector, propagation_matrix, noise_var, sliced_constellation, detection_sequence):
    blocks = propagation_matrix.shape[0]
    per_section = propagation_matrix.shape[1]
    users = propagation_matrix.shape[2]
    section_id = lax.axis_index("section")
    first = section_id * per_section
    padded = padded_2(propagation_matrix, (("sc", 0),), 1)
    smooth = 0.5 * padded[1:-1] + 0.25 * (padded[:-2] + padded[2:])
    basis_all = jnp.concatenate([smooth, rotate(smooth)], axis=2)
    every_code = lax.all_gather(sliced_constellation, "section", axis=2, tiled=True)
    group_count = every_code.shape[2] // users
    constellation_labels = jnp.take(
        every_code.reshape(blocks, every_code.shape[1], group_count, users),
        detection_sequence,
        axis=2,
    )
    symbols = symbol_values(constellation_labels)
    own_terms = []
    for slot in range(per_section):
        own_sym = lax.dynamic_index_in_dim(symbols, first + slot, 2, keepdims=False)
        own_terms.append(
            jnp.einsum("sti,sik->stk", own_sym, basis_all[:, slot], precision=lax.Precision.HIGHEST)
        )
    local_total = own_terms[0]
    for term in own_terms[1:]:
        local_total = local_total + term
    piece = lax.all_gather(smooth, "section", axis=1, tiled=True)
    count = piece.shape[1]
    piece_sym = symbols
    keep = (jnp.arange(count, dtype=jnp.int32) < first).astype(jnp.float32)
    piece_sym = piece_sym * keep[None, None, :, None]
    piece_basis = jnp.concatenate([piece, rotate(piece)], axis=2)
    earlier = jnp.einsum("stgi,sgik->stk", piece_sym, piece_basis, precision=lax.Precision.HIGHEST)
    current = observed_vector - earlier
    filters, amplitude_level = filter_block(basis_all, noise_var)
    totals = lax.psum(jnp.sum(amplitude_level, axis=0), "sc")
    average_amplitude = totals / (blocks * lax.axis_size("sc"))
    results = []
    for slot in range(per_section):
        scale = jnp.concatenate([average_amplitude[slot], average_amplitude[slot]])
        est = (
            jnp.einsum("sik,stk->sti", filters[:, slot], current, precision=lax.Precision.HIGHEST)
            / scale
        )
        results.append(est)
        current = current - own_terms[slot]
    output = jnp.concatenate(results, axis=2)
    return output


def solution(mesh):
    in_specs = (
        P("sc", None, None),
        P("sc", "section", None, None),
        P("sc"),
        P("sc", None, "section"),
        P(),
    )
    out_specs = P("sc", None, "section")
    return jax.shard_map(local, mesh=mesh, in_specs=in_specs, out_specs=out_specs, check_vma=False)
```

profile of v0, /device:TPU:0, one launch (start us, length us, event | category | flops | bytes accessed | tf_op | source)
XLA Modules:
  0.0 132.7 jit_solution(6204157626375704938)
XLA Ops:
  6.5 0.7 fusion.193
  7.2 1.3 collective-permute-start.1
  8.5 3.0 %collective-permute-start = (f32[1,2,4,128]{3,2,1,0:T(4,128)S(1)}, f32[1,2,4,128]{3,2,1,0:T(4,128)S(1)}, u32[]{:S(2)}, u32[]{:S(2)}) collective-permute-start(f32[1,2,4,128]{3,2,1,0:T(4,128)S(1)} %get-tuple-element.152), channel_id=1, source_target_pairs={{0,1},{1,2},{2,3},{3,4},{4,5},{5,6},{6,7},{8,9},{9,10},{10,11},{11... | collective-permute-start | bytes 12296 | tf_op jit(solution)/shard_map/ppermute | solution.py:16
  11.6 0.7 compare_select_fusion
  12.2 0.7 compare_and_fusion
  12.9 12.5 %all_gather.6 = s32[128,14,32]{0,2,1:T(8,128)S(1)} all-gather(s32[128,14,8]{0,2,1:T(8,128)} %param.8), channel_id=1, replica_groups=mesh['section'=4,'sc'=8] {'section'}, dimensions={2}, use_global_device_ids=true | all-gather | bytes 286720 | tf_op jit(solution)/shard_map/all_gather | solution.py:92
  25.4 0.7 gather_fusion
  26.1 0.6 fusion.25
  26.9 0.6 fusion.32
  27.5 0.2 broadcast_multiply_fusion
  27.7 4.5 %copy.2082 = f32[128,14,8,8]{1,3,2,0:T(8,128)} copy(f32[128,14,8,8]{0,3,1,2:T(8,128)S(1)} %fusion.21) | data formatting | bytes 917504 | tf_op jit(solution)/shard_map/mul | solution.py:113
  32.3 1.0 fusion.18
  33.3 1.6 %slice_negate_fusion.1 = (f32[128,2,4,64]{3,2,1,0:T(4,128)S(1)}, f32[128,2,4,64]{3,2,1,0:T(4,128)S(1)}) fusion(f32[128,2,4,128]{3,2,1,0:T(4,128)} %fusion.18), kind=kLoop, calls=%fused_computation.26 | loop fusion | flops 65536 | bytes 1048576 | tf_op jit(solution)/shard_map/neg | solution.py:24
  34.9 2.3 %convolution_add_fusion = f32[128,2,8,8]{3,2,1,0:T(8,128)S(1)} fusion(f32[128,8,8]{2,1,0:T(8,128)S(1)} %broadcast_multiply_fusion, f32[128,2,4,64]{3,2,1,0:T(4,128)S(1)} %get-tuple-element.151, f32[128,2,4,64]{3,2,1,0:T(4,128)S(1)} %get-tuple-element.150, f32[128,2,4,128]{3,2,1,0:T(4,128)S(1)} %copy-done), kind=kOutput, calls=%fused_computation.11 | convolution fusion | flops 25706496 | bytes 1146880 | tf_op jit(solution)/shard_map/sgik,sgjk->sgij/dot_general | solution.py:73
  37.2 4.3 %fusion.192 = (f32[128,2,1,1]{3,2,1,0:T(1,128)S(1)}, f32[128,2,1,1]{3,2,1,0:T(1,128)S(1)}, f32[128,2,1,1]{3,2,1,0:T(1,128)S(1)}, f32[128,2,1,1]{3,2,1,0:T(1,128)...) fusion(f32[128,2,8,8]{3,2,1,0:T(8,128)S(1)} %convolution_add_fusion), kind=kLoop, calls=%fused_computation.348 | loop fusion | bytes 34816 | tf_op jit(solution)/shard_map/slice | solution.py:35
  41.5 5.8 %fusion.191 = (f32[128,2,1,1]{3,2,1,0:T(1,128)S(1)}, f32[128,2,1,1]{3,2,1,0:T(1,128)}, f32[128,2,1,1]{3,2,1,0:T(1,128)}, f32[128,2,1,1]{3,2,1,0:T(1,128)}, f32[1...) fusion(f32[128,2,8,8]{3,2,1,0:T(8,128)S(1)} %convolution_add_fusion), kind=kLoop, calls=%fused_computation.347 | loop fusion | bytes 38912 | tf_op jit(solution)/shard_map/slice | solution.py:35
  47.3 1.0 copy.2176
  48.3 1.6 %copy.2156 = f32[128,2,1,1]{0,1,3,2:T(2,128)} copy(f32[128,2,1,1]{3,2,1,0:T(1,128)} %get-tuple-element.148) | data formatting | bytes 2048 | tf_op jit(solution)/shard_map/squeeze | solution.py:35
  49.8 1.5 %copy.2101 = f32[128,2,1,1]{0,1,3,2:T(2,128)} copy(f32[128,2,1,1]{3,2,1,0:T(1,128)} %get-tuple-element.141) | data formatting | bytes 2048 | tf_op jit(solution)/shard_map/slice | solution.py:35
  51.4 1.6 %copy.2158 = f32[128,2,1,1]{0,1,3,2:T(2,128)} copy(f32[128,2,1,1]{3,2,1,0:T(1,128)} %get-tuple-element.147) | data formatting | bytes 2048 | tf_op jit(solution)/shard_map/squeeze | solution.py:35
  52.9 1.5 %copy.2108 = f32[128,2,1,1]{0,1,3,2:T(2,128)} copy(f32[128,2,1,1]{3,2,1,0:T(1,128)} %get-tuple-element.136) | data formatting | bytes 2048 | tf_op jit(solution)/shard_map/slice | solution.py:35
  54.4 1.5 %copy.2095 = f32[128,2,1,1]{0,1,3,2:T(2,128)} copy(f32[128,2,1,1]{3,2,1,0:T(1,128)} %get-tuple-element.145) | data formatting | bytes 2048 | tf_op jit(solution)/shard_map/slice | solution.py:35
  56.0 1.6 %copy.2116 = f32[128,2,1,1]{0,1,3,2:T(2,128)} copy(f32[128,2,1,1]{3,2,1,0:T(1,128)} %get-tuple-element.129) | data formatting | bytes 2048 | tf_op jit(solution)/shard_map/slice | solution.py:35
  57.6 1.6 %copy.2125 = f32[128,2,1,1]{0,1,3,2:T(2,128)} copy(f32[128,2,1,1]{3,2,1,0:T(1,128)} %get-tuple-element.122) | data formatting | bytes 2048 | tf_op jit(solution)/shard_map/slice | solution.py:35
  59.1 1.0 copy.2134
  60.1 1.0 copy.2133
  61.1 1.6 %copy.2132 = f32[128,2,1,1]{0,1,3,2:T(2,128)} copy(f32[128,2,1,1]{3,2,1,0:T(1,128)} %get-tuple-element.117) | data formatting | bytes 2048 | tf_op jit(solution)/shard_map/slice | solution.py:35
  62.7 1.6 %copy.2131 = f32[128,2,1,1]{0,1,3,2:T(2,128)} copy(f32[128,2,1,1]{3,2,1,0:T(1,128)} %get-tuple-element.118) | data formatting | bytes 2048 | tf_op jit(solution)/shard_map/slice | solution.py:35
  64.2 1.5 %copy.2130 = f32[128,2,1,1]{0,1,3,2:T(2,128)} copy(f32[128,2,1,1]{3,2,1,0:T(1,128)} %get-tuple-element.119) | data formatting | bytes 2048 | tf_op jit(solution)/shard_map/slice | solution.py:35
  65.8 1.6 %copy.2129 = f32[128,2,1,1]{0,1,3,2:T(2,128)} copy(f32[128,2,1,1]{3,2,1,0:T(1,128)} %get-tuple-element.120) | data formatting | bytes 2048 | tf_op jit(solution)/shard_map/slice | solution.py:35
  67.4 1.6 %copy.2128 = f32[128,2,1,1]{0,1,3,2:T(2,128)} copy(f32[128,2,1,1]{3,2,1,0:T(1,128)} %get-tuple-element.121) | data formatting | bytes 2048 | tf_op jit(solution)/shard_map/slice | solution.py:35
  68.9 1.5 %copy.2124 = f32[128,2,1,1]{0,1,3,2:T(2,128)} copy(f32[128,2,1,1]{3,2,1,0:T(1,128)} %get-tuple-element.123) | data formatting | bytes 2048 | tf_op jit(solution)/shard_map/slice | solution.py:35
  70.4 1.5 %copy.2123 = f32[128,2,1,1]{0,1,3,2:T(2,128)} copy(f32[128,2,1,1]{3,2,1,0:T(1,128)} %get-tuple-element.124) | data formatting | bytes 2048 | tf_op jit(solution)/shard_map/slice | solution.py:35
  71.9 1.5 %copy.2122 = f32[128,2,1,1]{0,1,3,2:T(2,128)} copy(f32[128,2,1,1]{3,2,1,0:T(1,128)} %get-tuple-element.125) | data formatting | bytes 2048 | tf_op jit(solution)/shard_map/slice | solution.py:35
  73.5 1.5 %copy.2121 = f32[128,2,1,1]{0,1,3,2:T(2,128)} copy(f32[128,2,1,1]{3,2,1,0:T(1,128)} %get-tuple-element.126) | data formatting | bytes 2048 | tf_op jit(solution)/shard_map/slice | solution.py:35
  75.0 1.6 %copy.2120 = f32[128,2,1,1]{0,1,3,2:T(2,128)} copy(f32[128,2,1,1]{3,2,1,0:T(1,128)} %get-tuple-element.127) | data formatting | bytes 2048 | tf_op jit(solution)/shard_map/slice | solution.py:35
  76.5 1.6 %copy.2119 = f32[128,2,1,1]{0,1,3,2:T(2,128)} copy(f32[128,2,1,1]{3,2,1,0:T(1,128)} %get-tuple-element.128) | data formatting | bytes 2048 | tf_op jit(solution)/shard_map/slice | solution.py:35
  78.1 0.6 copy.2115
  80.0 0.7 bitcast_multiply_fusion.13
  80.7 0.9 constant_dynamic-update-slice_fusion.63
  82.5 0.2 copy.2144
  82.7 0.2 copy.2145
  82.8 0.1 copy.2146
  83.0 0.2 copy.2147
  83.2 0.2 copy.2148
  83.3 0.2 copy.2149
  83.5 0.8 copy.2150
  84.3 2.7 %stack.50 = f32[128,2,8,8]{3,2,1,0:T(8,128)S(1)} concatenate(f32[128,2,1,8]{3,2,1,0:T(1,128)S(1)} %copy.2143, f32[128,2,1,8]{3,2,1,0:T(1,128)S(1)} %copy.2144, f32[128,2,1,8]{3,2,1,0:T(1,128)S(1)} %copy.2145, f32[128,2,1,8]{3,2,1,0:T(1,128)S(1)} %copy.2146, f32[128,2,1,8]{3,2,1,0:T(1,128)S(1)} %copy.2147, f32[128,2,1,8]{3,2,1,0:T(1,128)S(1)} %copy.2148, ...), dimensions={2} | concatenate | bytes 131072 | tf_op jit(solution)/shard_map/stack | solution.py:66
  87.0 0.4 copy.2151
  87.4 0.6 gather_fusion.1
  88.1 1.1 copy.2152
  89.2 13.8 %psum.7 = f32[2,4]{0,1:T(4,128)S(1)} all-reduce(f32[2,4]{0,1:T(4,128)S(1)} %fusion.34), channel_id=1, replica_groups=mesh['section'=4,'sc'=8] {'sc'}, use_global_device_ids=true, to_apply=%region_1.2 | all-reduce | flops 8 | bytes 64 | tf_op jit(solution)/shard_map/psum | solution.py:118
  102.9 0.2 slice_reduce_fusion.1
  103.3 3.1 %fusion.20 = f32[128,2,8,128]{3,2,1,0:T(8,128)} fusion(f32[128,2,8,8]{3,2,1,0:T(8,128)S(1)} %stack.50, f32[128,2,4,64]{3,2,1,0:T(4,128)S(1)} %get-tuple-element.151, f32[128,2,4,64]{3,2,1,0:T(4,128)S(1)} %get-tuple-element.150, f32[128,2,4,128]{3,2,1,0:T(4,128)S(1)} %copy-done), kind=kOutput, calls=%fused_computation.33 | convolution fusion | flops 25690112 | bytes 2162688 | tf_op jit(solution)/shard_map/sgij,sgjk->sgik/dot_general | solution.py:77
  106.4 3.6 %slice_negate_fusion = (f32[128,8,4,64]{3,2,1,0:T(4,128)S(1)}, f32[128,8,4,64]{3,2,1,0:T(4,128)S(1)}) fusion(f32[128,8,4,128]{3,2,1,0:T(4,128)} %all-gather.2.cloned.1.call-done), kind=kLoop, calls=%fused_computation.8 | loop fusion | flops 262144 | bytes 4194304 | tf_op jit(solution)/shard_map/neg | solution.py:24
  110.0 0.4 copy-done.2
  110.5 0.2 copy-done.3
  110.7 8.3 %fusion.9 = f32[128,14,128]{2,1,0:T(8,128)S(1)} fusion(f32[128,14,8,8]{1,3,2,0:T(8,128)S(1)} %copy-done.2, f32[128,8,4,64]{3,2,1,0:T(4,128)S(1)} %get-tuple-element.113, f32[128,8,4,64]{3,2,1,0:T(4,128)S(1)} %get-tuple-element.112, f32[128,8,4,128]{3,2,1,0:T(4,128)S(1)} %copy-done.1, f32[128,14,128]{2,0,1:T(8,128)S(1)} %copy-done.3), kind=kOutput, calls=%fused_computation.12 | convolution fusion | flops 178487296 | bytes 6488064 | tf_op jit(solution)/shard_map/stgi,sgik->stk/dot_general | solution.py:115
  119.0 2.3 %convolution_subtract_fusion = f32[128,14,128]{2,1,0:T(8,128)S(1)} fusion(f32[128,14,128]{2,1,0:T(8,128)S(1)} %fusion.9, f32[128,2,4,128]{3,2,1,0:T(4,128)S(1)} %copy-done, f32[128,2,4,64]{3,2,1,0:T(4,128)S(1)} %get-tuple-element.151, f32[128,2,4,64]{3,2,1,0:T(4,128)S(1)} %get-tuple-element.150, f32[128,14,1,8]{1,3,0,2:T(8,128)S(1)} %copy.2152), kind=kOutput, calls=%fused_computation.10 | convolution fusion | flops 22511616 | bytes 2940928 | tf_op jit(solution)/shard_map/sti,sik->stk/dot_general | solution.py:104
  121.3 1.7 %convolution_divide_fusion = f32[128,14,8]{1,2,0:T(8,128)S(1)} fusion(f32[128,14,128]{2,1,0:T(8,128)S(1)} %convolution_subtract_fusion, f32[128,2,8,128]{3,2,1,0:T(8,128)S(1)} %copy-done.4, f32[8]{0:T(128)S(1)} %pad_maximum_fusion.5), kind=kOutput, calls=%fused_computation.13 | convolution fusion | flops 22034432 | bytes 1630720 | tf_op jit(solution)/shard_map/sik,stk->sti/dot_general | solution.py:124
  123.0 0.2 copy.2154
  123.3 1.7 %convolution_divide_fusion.1 = f32[128,14,8]{1,2,0:T(8,128)S(1)} fusion(f32[128,14,128]{2,1,0:T(8,128)S(1)} %fusion.9, f32[128,2,8,128]{3,2,1,0:T(8,128)S(1)} %copy-done.5, f32[8]{0:T(128)S(1)} %pad_maximum_fusion.4), kind=kOutput, calls=%fused_computation.14 | convolution fusion | flops 22034432 | bytes 1630720 | tf_op jit(solution)/shard_map/sik,stk->sti/dot_general | solution.py:124
  125.0 0.2 copy.2153
  125.2 0.7 pad_maximum_fusion.3
  (84 shorter events, 2.5 us)
Async XLA Ops:
  6.5 99.9 %all-gather.2.cloned.1.call-start = ((), (), s32[]{:S(2)}) async-start(), calls=%async_computation | async-start | bytes 2621440 | tf_op jit(solution)/shard_map/all_gather | solution.py:109
  7.2 25.0 %collective-permute-start.1 = (f32[1,2,4,128]{3,2,1,0:T(4,128)S(1)}, f32[1,2,4,128]{3,2,1,0:T(4,128)S(1)}, u32[]{:S(2)}, u32[]{:S(2)}) collective-permute-start(f32[1,2,4,128]{3,2,1,0:T(4,128)S(1)} %get-tuple-element.153), channel_id=1, source_target_pairs={{1,0},{2,1},{3,2},{4,3},{5,4},{6,5},{7,6},{9,8},{10,9},{11,10},{12... | collective-permute-start | bytes 12296 | tf_op jit(solution)/shard_map/ppermute | solution.py:17
  8.5 23.8 %collective-permute-start = (f32[1,2,4,128]{3,2,1,0:T(4,128)S(1)}, f32[1,2,4,128]{3,2,1,0:T(4,128)S(1)}, u32[]{:S(2)}, u32[]{:S(2)}) collective-permute-start(f32[1,2,4,128]{3,2,1,0:T(4,128)S(1)} %get-tuple-element.152), channel_id=1, source_target_pairs={{0,1},{1,2},{2,3},{3,4},{4,5},{5,6},{6,7},{8,9},{9,10},{10,11},{11... | collective-permute-start | bytes 12296 | tf_op jit(solution)/shard_map/ppermute | solution.py:16
  26.1 1.4 %copy-start.7 = (f32[128]{0:T(128)S(1)}, f32[128]{0:T(128)}, u32[]{:S(2)}) copy-start(f32[128]{0:T(128)} %param.7) | copy-start | bytes 1540
  27.7 4.6 %copy-start.6 = (f32[128,2,4,128]{3,2,1,0:T(4,128)S(1)}, f32[128,2,4,128]{3,2,1,0:T(4,128)}, u32[]{:S(2)}) copy-start(f32[128,2,4,128]{3,2,1,0:T(4,128)} %param.6) | copy-start | bytes 1572868
  33.3 1.6 %copy-start = (f32[128,2,4,128]{3,2,1,0:T(4,128)S(1)}, f32[128,2,4,128]{3,2,1,0:T(4,128)}, u32[]{:S(2)}) copy-start(f32[128,2,4,128]{3,2,1,0:T(4,128)} %fusion.18) | copy-start | bytes 1572868
  82.8 5.2 %copy-start.8 = (f32[128]{0:T(128)S(1)}, f32[128]{0:T(128)}, u32[]{:S(2)}) copy-start(f32[128]{0:T(128)} %param.7) | copy-start | bytes 1540
  106.4 3.6 %copy-start.1 = (f32[128,8,4,128]{3,2,1,0:T(4,128)S(1)}, f32[128,8,4,128]{3,2,1,0:T(4,128)}, u32[]{:S(2)}) copy-start(f32[128,8,4,128]{3,2,1,0:T(4,128)} %all-gather.2.cloned.1.call-done) | copy-start | bytes 6291460
  106.4 4.1 %copy-start.2 = (f32[128,14,8,8]{1,3,2,0:T(8,128)S(1)}, f32[128,14,8,8]{1,3,2,0:T(8,128)}, u32[]{:S(2)}) copy-start(f32[128,14,8,8]{1,3,2,0:T(8,128)} %copy.2082) | copy-start | bytes 1376260
  106.4 4.3 %copy-start.3 = (f32[128,14,128]{2,0,1:T(8,128)S(1)}, f32[128,14,128]{2,0,1:T(8,128)}, u32[]{:S(2)}) copy-start(f32[128,14,128]{2,0,1:T(8,128)} %param.5) | copy-start | bytes 2752516
  119.0 2.3 %copy-start.4 = (f32[128,2,8,128]{3,2,1,0:T(8,128)S(1)}, f32[128,2,8,128]{3,2,1,0:T(8,128)}, u32[]{:S(2)}) copy-start(f32[128,2,8,128]{3,2,1,0:T(8,128)} %fusion.20) | copy-start | bytes 3145732
  121.3 2.0 %copy-start.5 = (f32[128,2,8,128]{3,2,1,0:T(8,128)S(1)}, f32[128,2,8,128]{3,2,1,0:T(8,128)}, u32[]{:S(2)}) copy-start(f32[128,2,8,128]{3,2,1,0:T(8,128)} %fusion.20) | copy-start | bytes 3145732
Sparse Core Ops, SparseCore 0:
  33.4 34.1 all-gather.1
where the time goes:
time: 134 us; the launch traced here: 133 us
  local copies, waits for them, and re-layouts  56.8 us (42%)
  blocking collectives  26.2 us (20%)
  matrix products  19.5 us (15%)
  between operations  13.8 us (10%)
  other arithmetic  12.1 us (9%)
  starting transfers between devices  4.31 us (3%)
    slice x33, local copies, waits for them, and re-layouts, invert_small(): entry = [[gram[..., i, j] for j in range(width)] for i in range(width)]  38.5 us
    psum x1, blocking collectives, local(): totals = lax.psum(jnp.sum(amplitude_level, axis=0), 'sc')  13.8 us
    all_gather x1, blocking collectives, local(): lax.all_gather(sliced_constellation, 'section', axis=2, tiled=True)  12.5 us
    dot_general x1, matrix products, local(): jnp.einsum('stgi,sgik->stk', piece_sym, piece_basis, precision=lax.Precis...  8.29 us
    neg x2, other arithmetic, rotate(): return jnp.concatenate([-vectors[..., half:], vectors[..., :half]], axis=-1)  5.22 us
    another operation x10, local copies, waits for them, and re-layouts, invert_small(): return jnp.stack(rows, axis=-2)  4.98 us
    mul x1, local copies, waits for them, and re-layouts, local(): piece_sym = piece_sym * keep[None, None, :, None]  4.54 us
    dot_general x2, matrix products, local(): jnp.einsum('sik,stk->sti', filters[:, slot], current, precision=lax.Preci...  3.49 us
  transfers between devices with their start and end apart: 3, of which 0 were waited for; matrix products, arithmetic and copies ran while one was open for 51% of the time, Pallas kernels for 0%

commit v1 on v0

v1 whole, which is shorter than its diff:
```python
import functools

import jax
import jax.numpy as jnp
from jax import lax
from jax.experimental import pallas as pl
from jax.experimental.pallas import tpu as pltpu
from jax.sharding import PartitionSpec as P

ROOT_TEN = 3.1622776601683795
LANES = 128


def c_mul(a, b):
    return (a[0] * b[0] - a[1] * b[1], a[0] * b[1] + a[1] * b[0])


def c_mul_conj(a, b):
    return (a[0] * b[0] + a[1] * b[1], a[1] * b[0] - a[0] * b[1])


def c_add(a, b):
    return (a[0] + b[0], a[1] + b[1])


def c_sub(a, b):
    return (a[0] - b[0], a[1] - b[1])


def invert_hermitian(entry, width):
    low = [[None] * width for _ in range(width)]
    recip = [None] * width
    for j in range(width):
        pivot = entry[j][j][0]
        for k in range(j):
            pivot = pivot - (low[j][k][0] * low[j][k][0] + low[j][k][1] * low[j][k][1])
        recip[j] = 1.0 / jnp.sqrt(pivot)
        for i in range(j + 1, width):
            value = entry[i][j]
            for k in range(j):
                value = c_sub(value, c_mul_conj(low[i][k], low[j][k]))
            low[i][j] = (value[0] * recip[j], value[1] * recip[j])
    inv_low = [[None] * width for _ in range(width)]
    zero = jnp.zeros_like(recip[0])
    for i in range(width):
        inv_low[i][i] = (recip[i], zero)
        for j in range(i):
            value = (low[i][j][0] * recip[j], low[i][j][1] * recip[j])
            for k in range(j + 1, i):
                value = c_add(value, c_mul(low[i][k], inv_low[k][j]))
            inv_low[i][j] = (-value[0] * recip[i], -value[1] * recip[i])
    inverse = [[None] * width for _ in range(width)]
    for i in range(width):
        for j in range(i + 1):
            value = c_mul_conj(inv_low[i][j], inv_low[i][i])
            for k in range(i + 1, width):
                value = c_add(value, c_mul_conj(inv_low[k][j], inv_low[k][i]))
            inverse[i][j] = value
            if i != j:
                inverse[j][i] = (value[0], -value[1])
    return inverse


def kernel(
    dims, det_ref, y_hbm, h_hbm, noise_ref, code_ref, out_ref,
    hsend, hbuf, ybuf, stage, csend, cbuf, pscr, tscr, sre, sim, gsend, gbuf, rsend, rbuf,
    load_sem, send_h, recv_h, send_c, recv_c, send_e, recv_lo, recv_hi, send_g, recv_g, send_r, recv_r,
):
    n, nc, tones, slots, users, times = dims
    total = n * nc
    rows = slots * users
    all_users = n * rows
    positions = n * slots
    fl = tones // n
    gb = LANES // users
    fb = min(gb, fl)
    repeats = gb // fb
    chunks = fl // fb
    tp = stage.shape[0] // rows
    tiles = pscr.shape[0]
    width = tiles * LANES
    half = h_hbm.shape[-1] // 2

    s = lax.axis_index("section")
    c = lax.axis_index("sc")
    me = s * nc + c

    def at(section, sc):
        return {"section": section, "sc": sc}

    def remote(src, dst, send, recv, section, sc):
        return pltpu.make_async_remote_copy(
            src_ref=src, dst_ref=dst, send_sem=send, recv_sem=recv,
            device_id=at(section, sc), device_id_type=pl.DeviceIdType.MESH,
        )

    load_h = pltpu.make_async_copy(h_hbm, hsend, load_sem.at[0])
    load_h.start()
    load_y = pltpu.make_async_copy(
        y_hbm.at[:, pl.ds(pl.multiple_of(s * fl, 8), fl), :], ybuf, load_sem.at[1]
    )
    load_y.start()

    barrier = pltpu.get_barrier_semaphore()

    def greet(d, carry):
        other = lax.rem(me + d, total)
        pl.semaphore_signal(
            barrier, inc=1, device_id=at(lax.div(other, nc), lax.rem(other, nc)),
            device_id_type=pl.DeviceIdType.MESH,
        )
        return carry

    lax.fori_loop(1, total, greet, 0)

    def span(m):
        lo, hi = max(m * fl - 1, 0), min(m * fl + fl + 1, tones)
        return lo, hi, lo - (m * fl - 1)

    for m in range(n):
        lo, hi, off = span(m)

        @pl.when(s == m)
        def _():
            pltpu.make_async_copy(
                h_hbm.at[lo:hi], hbuf.at[m, off : off + hi - lo], load_sem.at[2]
            ).start()

    stage[...] = jnp.zeros_like(stage)
    for g in range(rows):
        stage[pl.ds(g * tp, times), :] = code_ref[:, g, :].astype(jnp.float32)
    csend[...] = stage[...].T
    cbuf[s] = csend[pl.ds(pl.multiple_of(s * fl, 8), fl), :]

    @pl.when((s == 0) & (c == 0))
    def _():
        hbuf[:, 0] = jnp.zeros_like(hbuf[:, 0])

    @pl.when((s == n - 1) & (c == nc - 1))
    def _():
        hbuf[:, fl + 1] = jnp.zeros_like(hbuf[:, 0])

    load_h.wait()
    pl.semaphore_wait(barrier, total - 1)

    def main_copy(m, src_section):
        lo, hi, off = span(m)
        return remote(
            hsend.at[lo:hi], hbuf.at[src_section, off : off + hi - lo],
            send_h.at[m], recv_h.at[src_section], m, c,
        )

    def code_copy(m, src_section):
        return remote(
            csend.at[m * fl : (m + 1) * fl], cbuf.at[src_section],
            send_c.at[m], recv_c.at[src_section], m, c,
        )

    def high_copy(src_section):
        return remote(
            hsend.at[0], hbuf.at[src_section, fl + 1], send_e.at[0], recv_hi.at[src_section],
            n - 1, lax.rem(c + nc - 1, nc),
        )

    def low_copy(src_section):
        return remote(
            hsend.at[tones - 1], hbuf.at[src_section, 0], send_e.at[1], recv_lo.at[src_section],
            0, lax.rem(c + 1, nc),
        )

    @pl.when(c > 0)
    def _():
        high_copy(s).start()

    @pl.when(c < nc - 1)
    def _():
        low_copy(s).start()

    for m in range(n):

        @pl.when(s != m)
        def _():
            main_copy(m, s).start()

    for m in range(n):

        @pl.when(s != m)
        def _():
            code_copy(m, s).start()

    load_y.wait()
    for m in range(n):
        lo, hi, off = span(m)

        @pl.when(s == m)
        def _():
            pltpu.make_async_copy(
                h_hbm.at[lo:hi], hbuf.at[m, off : off + hi - lo], load_sem.at[2]
            ).wait()
            for src in range(n):
                if src != m:
                    main_copy(m, src).wait_recv()

    @pl.when((s == n - 1) & (c < nc - 1))
    def _():
        for src in range(n):
            high_copy(src).wait_recv()

    @pl.when((s == 0) & (c > 0))
    def _():
        for src in range(n):
            low_copy(src).wait_recv()

    lane = lax.broadcasted_iota(jnp.int32, (1, LANES), 1)
    turn = jnp.where(lane < half, -1.0, 1.0).astype(jnp.float32)

    def rotate(v):
        return pltpu.roll(v, half, 1) * turn

    def products(f, carry):
        parts = []
        for src in range(n):
            parts.append(
                0.5 * hbuf[src, f + 1] + 0.25 * (hbuf[src, f] + hbuf[src, f + 2])
            )
        h = jnp.concatenate(parts, axis=0)
        yf = ybuf[:, pl.ds(f, 1), :].reshape(times, LANES)
        yf = jnp.concatenate([yf, jnp.zeros((tp - times, LANES), jnp.float32)], axis=0)
        pieces = [h, rotate(h), yf, -rotate(yf)]
        spare = width - 2 * all_users - 2 * tp
        if spare:
            pieces.append(jnp.zeros((spare, LANES), jnp.float32))
        other = jnp.concatenate(pieces, axis=0)
        prod = lax.dot_general(
            h, other, (((1,), (1,)), ((), ())),
            precision=lax.Precision.HIGHEST, preferred_element_type=jnp.float32,
        )
        for k in range(tiles):
            pscr[k, pl.ds(pl.multiple_of(f * all_users, 8), all_users), :] = prod[
                :, k * LANES : (k + 1) * LANES
            ]
        return carry

    lax.fori_loop(0, fl, products, 0, unroll=4)

    gain_total = None
    weights = []
    for ch in range(chunks):
        for p in range(positions):
            for k in range(tiles):
                blk = jnp.concatenate(
                    [
                        pscr[k, pl.ds(ch * fb * all_users + p * users + u, fb, stride=all_users), :]
                        for u in range(users)
                        for _ in range(repeats)
                    ],
                    axis=0,
                )
                tscr[ch, pl.ds(p * width + k * LANES, LANES), :] = blk.T
        offset = s * fl + ch * fb
        row = lax.div(offset, LANES)
        shift = lax.rem(LANES - lax.rem(offset, LANES), LANES)
        noise = jnp.broadcast_to(noise_ref[pl.ds(row, 1), :], (8, LANES))
        noise = jnp.where(lane < fb, pltpu.roll(noise, shift, 1), 0.0)
        base = noise
        for b in range(1, users * repeats):
            noise = noise + pltpu.roll(base, fb * b, 1)
        if positions > 8:
            noise = jnp.concatenate([noise] * (positions // 8), axis=0)
        noise = noise[:positions]
        step = width + users
        d_re = [tscr[ch, pl.ds(v, positions, stride=step), :] for v in range(users)]
        d_im = [tscr[ch, pl.ds(all_users + v, positions, stride=step), :] for v in range(users)]

        def group(x, u):
            return x if u == 0 else pltpu.roll(x, LANES - gb * u, 1)

        entry = [[None] * users for _ in range(users)]
        for i in range(users):
            for j in range(i + 1):
                entry[i][j] = (group(d_re[j], i), -group(d_im[j], i))
            entry[i][i] = (entry[i][i][0] + noise, None)
        inverse = invert_hermitian(entry, users)

        def spread(values):
            result = None
            for u in range(users):
                moved = values[u] if u == 0 else pltpu.roll(values[u], gb * u, 1)
                result = moved if u == 0 else jnp.where(lane < gb * u, result, moved)
            return result

        weight = []
        for d in range(users):
            weight.append(
                (
                    spread([inverse[u][(u - d) % users][0] for u in range(users)]),
                    spread([inverse[u][(u - d) % users][1] for u in range(users)]),
                )
            )
        weights.append(weight)
        gain = 1.0 - noise * weight[0][0]
        gain_total = gain if gain_total is None else gain_total + gain

    for sp in range(n):
        gsend[sp] = gain_total[sp * slots : (sp + 1) * slots]
    gbuf[me] = gsend[s]

    def send_gain(d, carry):
        other = lax.rem(me + d, total)
        section = lax.div(other, nc)
        remote(gsend.at[section], gbuf.at[me], send_g, recv_g, section, lax.rem(other, nc)).start()
        return carry

    lax.fori_loop(1, total, send_gain, 0)

    for m in range(n):

        @pl.when(s == m)
        def _():
            for src in range(n):
                if src != m:
                    code_copy(m, src).wait_recv()

    for ch in range(chunks):
        for src in range(n):
            blk = cbuf[src, ch * fb : (ch + 1) * fb, :]
            codes = jnp.concatenate([blk] * (users * repeats), axis=0).T
            high = jnp.floor(codes * 0.25)
            re = (2.0 * (codes - 4.0 * high) - 3.0) / ROOT_TEN
            im = (2.0 * high - 3.0) / ROOT_TEN
            for slot in range(slots):
                part = slice(slot * users * tp, (slot + 1) * users * tp)
                sre[ch, src * slots + slot] = re[part]
                sim[ch, src * slots + slot] = im[part]

    for ch in range(chunks):
        for p in range(positions):
            start = p * width
            z_re = tscr[ch, pl.ds(start + 2 * all_users, tp), :]
            z_im = tscr[ch, pl.ds(start + 2 * all_users + tp, tp), :]
            for q in range(p):
                g = det_ref[q]
                for v in range(users):
                    g_re = tscr[ch, pl.ds(start + q * users + v, 1), :]
                    g_im = tscr[ch, pl.ds(start + all_users + q * users + v, 1), :]
                    s_re = sre[ch, g, v * tp : (v + 1) * tp, :]
                    s_im = sim[ch, g, v * tp : (v + 1) * tp, :]
                    z_re = z_re - (g_re * s_re + g_im * s_im)
                    z_im = z_im - (g_re * s_im - g_im * s_re)
            x_re = None
            for d in range(users):
                w_re = weights[ch][d][0][p : p + 1]
                w_im = weights[ch][d][1][p : p + 1]
                r_re = z_re if d == 0 else pltpu.roll(z_re, gb * d, 1)
                r_im = z_im if d == 0 else pltpu.roll(z_im, gb * d, 1)
                t_re = w_re * r_re - w_im * r_im
                t_im = w_re * r_im + w_im * r_re
                x_re = t_re if d == 0 else x_re + t_re
                x_im = t_im if d == 0 else x_im + t_im
            rsend[p // slots, ch, p % slots, 0] = x_re
            rsend[p // slots, ch, p % slots, 1] = x_im

    def result_copy(m, src_section):
        return remote(
            rsend.at[m], rbuf.at[src_section], send_r.at[m], recv_r.at[src_section], m, c
        )

    for m in range(n):

        @pl.when(s != m)
        def _():
            result_copy(m, s).start()

    rbuf[s] = rsend[s]

    gain_wait = remote(gbuf.at[0 : total - 1], gbuf.at[0 : total - 1], send_g, recv_g, s, c)
    gain_wait.wait_recv()
    gain_sum = jnp.sum(gbuf[...], axis=0)
    recip = []
    for u in range(users):
        own = (lane >= gb * u) & (lane < gb * (u + 1))
        mean = jnp.sum(jnp.where(own, gain_sum, 0.0), axis=1, keepdims=True) / (tones * nc * repeats)
        recip.append(1.0 / mean)

    for m in range(n):

        @pl.when(s != m)
        def _():
            result_copy(m, m).wait_recv()

    for tile in range(tones // LANES):
        for slot in range(slots):
            for ri in range(2):
                blocks = []
                for b in range(users * repeats):
                    g = tile * users * repeats + b
                    blocks.append(rbuf[g // chunks, g % chunks, slot, ri])
                for u in range(users):
                    value = None
                    for b in range(users * repeats):
                        move = (gb * (b // repeats - u)) % LANES
                        moved = pltpu.roll(blocks[b], move, 1) if move else blocks[b]
                        value = moved if b == 0 else jnp.where(lane < fb * b, value, moved)
                    value = value * recip[u][slot : slot + 1]
                    out_ref[:, slot * 2 * users + ri * users + u, tile * LANES : (tile + 1) * LANES] = value[:times]

    @pl.when(c > 0)
    def _():
        high_copy(s).wait_send()

    @pl.when(c < nc - 1)
    def _():
        low_copy(s).wait_send()

    for m in range(n):

        @pl.when(s != m)
        def _():
            main_copy(m, s).wait_send()
            code_copy(m, s).wait_send()
            result_copy(m, s).wait_send()

    gain_wait.wait_send()


def local(observed_vector, propagation_matrix, noise_var, sliced_constellation, detection_sequence):
    n, nc = lax.axis_size("section"), lax.axis_size("sc")
    tones, slots, users, depth = propagation_matrix.shape
    times = observed_vector.shape[1]
    rows = slots * users
    all_users = n * rows
    positions = n * slots
    fl = tones // n
    chunks = max(fl // (LANES // users), 1)
    tp = -(-times // 8) * 8
    tiles = -(-(2 * all_users + 2 * tp) // LANES)
    dims = (n, nc, tones, slots, users, times)
    f32 = jnp.float32
    vmem = pl.BlockSpec(memory_space=pltpu.VMEM)
    hbm = pl.BlockSpec(memory_space=pl.ANY)
    dma = pltpu.SemaphoreType.DMA
    out = pl.pallas_call(
        functools.partial(kernel, dims),
        out_shape=jax.ShapeDtypeStruct((times, 2 * rows, tones), f32),
        in_specs=[pl.BlockSpec(memory_space=pltpu.SMEM), hbm, hbm, vmem, vmem],
        out_specs=vmem,
        scratch_shapes=[
            pltpu.VMEM((tones, rows, depth), f32),
            pltpu.VMEM((n, fl + 2, rows, depth), f32),
            pltpu.VMEM((times, fl, depth), f32),
            pltpu.VMEM((rows * tp, tones), f32),
            pltpu.VMEM((tones, rows * tp), f32),
            pltpu.VMEM((n, fl, rows * tp), f32),
            pltpu.VMEM((tiles, fl * all_users, LANES), f32),
            pltpu.VMEM((chunks, positions * tiles * LANES, LANES), f32),
            pltpu.VMEM((chunks, positions, users * tp, LANES), f32),
            pltpu.VMEM((chunks, positions, users * tp, LANES), f32),
            pltpu.VMEM((n, slots, LANES), f32),
            pltpu.VMEM((n * nc, slots, LANES), f32),
            pltpu.VMEM((n, chunks, slots, 2, tp, LANES), f32),
            pltpu.VMEM((n, chunks, slots, 2, tp, LANES), f32),
            dma((3,)),
            dma((n,)), dma((n,)),
            dma((n,)), dma((n,)),
            dma((2,)), dma((n,)), dma((n,)),
            dma, dma,
            dma((n,)), dma((n,)),
        ],
        compiler_params=pltpu.CompilerParams(collective_id=0, has_side_effects=True),
    )(
        detection_sequence,
        jnp.transpose(observed_vector, (1, 0, 2)),
        propagation_matrix.reshape(tones, rows, depth),
        noise_var.reshape(tones // LANES, LANES),
        jnp.transpose(sliced_constellation, (1, 2, 0)),
    )
    return jnp.transpose(out, (2, 0, 1))


def solution(mesh):
    in_specs = (
        P("sc", None, None),
        P("sc", "section", None, None),
        P("sc"),
        P("sc", None, "section"),
        P(),
    )
    out_specs = P("sc", None, "section")
    return jax.shard_map(local, mesh=mesh, in_specs=in_specs, out_specs=out_specs, check_vma=False)
```

time: 134 us -> 28.4 us (0.21)
  local copies, waits for them, and re-layouts: 56.8 us -> 1.55 us
  Pallas kernels: 0 us -> 26.6 us
  blocking collectives: 26.2 us -> 0 us
  matrix products: 19.5 us -> 0 us
  between operations: 13.8 us -> 0.01 us
  other arithmetic: 12.1 us -> 0 us
  starting transfers between devices: 4.31 us -> 0 us
    slice x35 -> x0, local copies, waits for them, and re-layouts: 39.4 us -> none  [the longest x33 38.5 us: invert_small(): entry = [[gram[..., i, j] for j in range(width)] for i in range(width)]]
    pallas_call x0 -> x1, Pallas kernels: none -> 26.6 us  [local(): pl.pallas_call(functools.partial(kernel, dims), out_shape=jax.ShapeDtypeS...]
    dot_general x6 -> x0, matrix products: 19.5 us -> none  [the longest x1 8.29 us: local(): jnp.einsum('stgi,sgik->stk', piece_sym, piece_basis, precision=lax.Precis...]
    psum x1 -> x0, blocking collectives: 13.8 us -> none  [local(): totals = lax.psum(jnp.sum(amplitude_level, axis=0), 'sc')]
    all_gather x1 -> x0, blocking collectives: 12.5 us -> none  [local(): lax.all_gather(sliced_constellation, 'section', axis=2, tiled=True)]
    neg x2 -> x0, other arithmetic: 5.22 us -> none  [rotate(): return jnp.concatenate([-vectors[..., half:], vectors[..., :half]], axis=-1)]
    another operation x10 -> x0, local copies, waits for them, and re-layouts: 4.98 us -> none  [invert_small(): return jnp.stack(rows, axis=-2)]
    mul x1 -> x0, local copies, waits for them, and re-layouts: 4.54 us -> none  [local(): piece_sym = piece_sym * keep[None, None, :, None]]
  transfers between devices with their start and end apart: 3 -> 0, of which waited for: 0 -> 0; matrix products, arithmetic and copies ran while one was open for 51% -> 0% of each run, Pallas kernels for 0% -> 0%
where the time goes in v1:
time: 28.4 us; the launch traced here: 28.2 us
  Pallas kernels  26.6 us (94%)
  local copies, waits for them, and re-layouts  1.55 us (5%)
    pallas_call x1, Pallas kernels, local(): pl.pallas_call(functools.partial(kernel, dims), out_shape=jax.ShapeDtypeS...  26.6 us
    unnamed x1, local copies, waits for them, and re-layouts  1.55 us

profile of v1, /device:TPU:0, one launch (start us, length us, event | category | flops | bytes accessed | tf_op | source)
XLA Modules:
  0.0 28.2 jit_solution(17373808528451076927)
XLA Ops:
  0.0 26.6 %shard_map.55 = f32[14,16,128]{2,1,0:T(8,128)} custom-call(s32[8]{0:T(128)} %det_ref.1, f32[14,128,128]{2,1,0:T(8,128)} %bitcast.5, f32[128,8,128]{2,1,0:T(8,128)} %bitcast.6, f32[1,128]{1,0:T(1,128)} %bitcast.9, s32[14,8,128]{2,1,0:T(8,128)} %bitcast.8), custom_call_target="tpu_custom_call" | custom-call | tf_op jit(solution)/shard_map/pallas_call | solution.py:442
  26.6 1.6 %copy.7 = f32[128,14,16]{0,2,1:T(8,128)} copy(f32[128,14,16]{0,2,1:T(8,128)} %bitcast.7) | data formatting | bytes 229376

commit v2 on v1

--- a/solution.py
+++ b/solution.py
@@ -103,15 +103,25 @@
 
     barrier = pltpu.get_barrier_semaphore()
 
-    def greet(d, carry):
-        other = lax.rem(me + d, total)
+    def wrap(value, size):
+        return jnp.where(value >= size, value - size, value)
+
+    def for_others(act):
+        for ds in reversed(range(n)):
+            section = wrap(s + ds, n)
+
+            def body(d, carry):
+                act(section, wrap(c + d, nc))
+                return carry
+
+            lax.fori_loop(0 if ds else 1, nc, body, 0, unroll=True if nc <= 8 else 4)
+
+    def greet(section, sc):
         pl.semaphore_signal(
-            barrier, inc=1, device_id=at(lax.div(other, nc), lax.rem(other, nc)),
-            device_id_type=pl.DeviceIdType.MESH,
-        )
-        return carry
-
-    lax.fori_loop(1, total, greet, 0)
+            barrier, inc=1, device_id=at(section, sc), device_id_type=pl.DeviceIdType.MESH
+        )
+
+    for_others(greet)
 
     def span(m):
         lo, hi = max(m * fl - 1, 0), min(m * fl + fl + 1, tones)
@@ -143,11 +153,17 @@
     load_h.wait()
     pl.semaphore_wait(barrier, total - 1)
 
-    def main_copy(m, src_section):
+    pieces_of = send_h.shape[1]
+    part = fl // pieces_of
+
+    def main_copy(m, src_section, k):
         lo, hi, off = span(m)
+        first = max(off, k * part + 2 if k else 0)
+        last = min(off + hi - lo, (k + 1) * part + 2)
+        start = m * fl - 1
         return remote(
-            hsend.at[lo:hi], hbuf.at[src_section, off : off + hi - lo],
-            send_h.at[m], recv_h.at[src_section], m, c,
+            hsend.at[start + first : start + last], hbuf.at[src_section, first:last],
+            send_h.at[m, k], recv_h.at[src_section, k], m, c,
         )
 
     def code_copy(m, src_section):
@@ -176,40 +192,14 @@
     def _():
         low_copy(s).start()
 
-    for m in range(n):
-
-        @pl.when(s != m)
-        def _():
-            main_copy(m, s).start()
-
-    for m in range(n):
-
-        @pl.when(s != m)
-        def _():
-            code_copy(m, s).start()
-
-    load_y.wait()
-    for m in range(n):
-        lo, hi, off = span(m)
-
-        @pl.when(s == m)
-        def _():
-            pltpu.make_async_copy(
-                h_hbm.at[lo:hi], hbuf.at[m, off : off + hi - lo], load_sem.at[2]
-            ).wait()
-            for src in range(n):
-                if src != m:
-                    main_copy(m, src).wait_recv()
-
-    @pl.when((s == n - 1) & (c < nc - 1))
-    def _():
-        for src in range(n):
-            high_copy(src).wait_recv()
-
-    @pl.when((s == 0) & (c > 0))
-    def _():
-        for src in range(n):
-            low_copy(src).wait_recv()
+    for k in range(pieces_of):
+        for m in range(n):
+
+            @pl.when(s != m)
+            def _():
+                main_copy(m, s, k).start()
+                if k == 0:
+                    code_copy(m, s).start()
 
     lane = lax.broadcasted_iota(jnp.int32, (1, LANES), 1)
     turn = jnp.where(lane < half, -1.0, 1.0).astype(jnp.float32)
@@ -241,7 +231,58 @@
             ]
         return carry
 
-    lax.fori_loop(0, fl, products, 0, unroll=4)
+    def make_symbols():
+        for m in range(n):
+
+            @pl.when(s == m)
+            def _():
+                for src in range(n):
+                    if src != m:
+                        code_copy(m, src).wait_recv()
+
+        for ch in range(chunks):
+            for src in range(n):
+                blk = cbuf[src, ch * fb : (ch + 1) * fb, :]
+                codes = jnp.concatenate([blk] * (users * repeats), axis=0).T
+                high = jnp.floor(codes * 0.25)
+                re = (2.0 * (codes - 4.0 * high) - 3.0) / ROOT_TEN
+                im = (2.0 * high - 3.0) / ROOT_TEN
+                for slot in range(slots):
+                    own = slice(slot * users * tp, (slot + 1) * users * tp)
+                    sre[ch, src * slots + slot] = re[own]
+                    sim[ch, src * slots + slot] = im[own]
+
+    load_y.wait()
+
+    @pl.when((s == 0) & (c > 0))
+    def _():
+        for src in range(n):
+            low_copy(src).wait_recv()
+
+    for k in range(pieces_of):
+        for m in range(n):
+            lo, hi, off = span(m)
+
+            @pl.when(s == m)
+            def _():
+                if k == 0:
+                    pltpu.make_async_copy(
+                        h_hbm.at[lo:hi], hbuf.at[m, off : off + hi - lo], load_sem.at[2]
+                    ).wait()
+                for src in range(n):
+                    if src != m:
+                        main_copy(m, src, k).wait_recv()
+
+        if k == pieces_of - 1:
+
+            @pl.when((s == n - 1) & (c < nc - 1))
+            def _():
+                for src in range(n):
+                    high_copy(src).wait_recv()
+
+        lax.fori_loop(k * part, (k + 1) * part, products, 0, unroll=min(8, part))
+        if k == pieces_of // 2 - 1:
+            make_symbols()
 
     gain_total = None
     weights = []
@@ -305,36 +346,18 @@
         gsend[sp] = gain_total[sp * slots : (sp + 1) * slots]
     gbuf[me] = gsend[s]
 
-    def send_gain(d, carry):
-        other = lax.rem(me + d, total)
-        section = lax.div(other, nc)
-        remote(gsend.at[section], gbuf.at[me], send_g, recv_g, section, lax.rem(other, nc)).start()
-        return carry
-
-    lax.fori_loop(1, total, send_gain, 0)
-
-    for m in range(n):
-
-        @pl.when(s == m)
-        def _():
-            for src in range(n):
-                if src != m:
-                    code_copy(m, src).wait_recv()
-
-    for ch in range(chunks):
-        for src in range(n):
-            blk = cbuf[src, ch * fb : (ch + 1) * fb, :]
-            codes = jnp.concatenate([blk] * (users * repeats), axis=0).T
-            high = jnp.floor(codes * 0.25)
-            re = (2.0 * (codes - 4.0 * high) - 3.0) / ROOT_TEN
-            im = (2.0 * high - 3.0) / ROOT_TEN
-            for slot in range(slots):
-                part = slice(slot * users * tp, (slot + 1) * users * tp)
-                sre[ch, src * slots + slot] = re[part]
-                sim[ch, src * slots + slot] = im[part]
-
-    for ch in range(chunks):
-        for p in range(positions):
+    def send_gain(section, sc):
+        remote(gsend.at[section], gbuf.at[me], send_g, recv_g, section, sc).start()
+
+    for_others(send_gain)
+
+    def result_copy(m, src_section):
+        return remote(
+            rsend.at[m], rbuf.at[src_section], send_r.at[m], recv_r.at[src_section], m, c
+        )
+
+    for p in range(positions):
+        for ch in range(chunks):
             start = p * width
             z_re = tscr[ch, pl.ds(start + 2 * all_users, tp), :]
             z_im = tscr[ch, pl.ds(start + 2 * all_users + tp, tp), :]
@@ -359,17 +382,12 @@
                 x_im = t_im if d == 0 else x_im + t_im
             rsend[p // slots, ch, p % slots, 0] = x_re
             rsend[p // slots, ch, p % slots, 1] = x_im
-
-    def result_copy(m, src_section):
-        return remote(
-            rsend.at[m], rbuf.at[src_section], send_r.at[m], recv_r.at[src_section], m, c
-        )
-
-    for m in range(n):
-
-        @pl.when(s != m)
-        def _():
-            result_copy(m, s).start()
+        if p % slots == slots - 1:
+
+            @pl.when(s != p // slots)
+            def _():
+                result_copy(p // slots, s).start()
+
 
     rbuf[s] = rsend[s]
 
@@ -416,7 +434,8 @@
 
         @pl.when(s != m)
         def _():
-            main_copy(m, s).wait_send()
+            for k in range(pieces_of):
+                main_copy(m, s, k).wait_send()
             code_copy(m, s).wait_send()
             result_copy(m, s).wait_send()
 
@@ -434,6 +453,7 @@
     chunks = max(fl // (LANES // users), 1)
     tp = -(-times // 8) * 8
     tiles = -(-(2 * all_users + 2 * tp) // LANES)
+    pieces_of = 4 if fl % 16 == 0 else 1
     dims = (n, nc, tones, slots, users, times)
     f32 = jnp.float32
     vmem = pl.BlockSpec(memory_space=pltpu.VMEM)
@@ -460,7 +480,7 @@
             pltpu.VMEM((n, chunks, slots, 2, tp, LANES), f32),
             pltpu.VMEM((n, chunks, slots, 2, tp, LANES), f32),
             dma((3,)),
-            dma((n,)), dma((n,)),
+            dma((n, pieces_of)), dma((n, pieces_of)),
             dma((n,)), dma((n,)),
             dma((2,)), dma((n,)), dma((n,)),
             dma, dma,

time: 28.4 us -> 25.2 us (0.89)
  Pallas kernels: 26.6 us -> 23.4 us
    pallas_call x1, Pallas kernels: 26.6 us -> 23.4 us  [local(): pl.pallas_call(functools.partial(kernel, dims), out_shape=jax.ShapeDtypeS...]
where the time goes in v2:
time: 25.2 us; the launch traced here: 25 us
  Pallas kernels  23.4 us (93%)
  local copies, waits for them, and re-layouts  1.55 us (6%)
    pallas_call x1, Pallas kernels, local(): pl.pallas_call(functools.partial(kernel, dims), out_shape=jax.ShapeDtypeS...  23.4 us
    unnamed x1, local copies, waits for them, and re-layouts  1.55 us

profile of v2, /device:TPU:0, one launch (start us, length us, event | category | flops | bytes accessed | tf_op | source)
XLA Modules:
  0.0 25.0 jit_solution(17582468794769080833)
XLA Ops:
  0.0 23.4 %shard_map.55 = f32[14,16,128]{2,1,0:T(8,128)} custom-call(s32[8]{0:T(128)} %det_ref.1, f32[14,128,128]{2,1,0:T(8,128)} %bitcast.5, f32[128,8,128]{2,1,0:T(8,128)} %bitcast.6, f32[1,128]{1,0:T(1,128)} %bitcast.9, s32[14,8,128]{2,1,0:T(8,128)} %bitcast.8), custom_call_target="tpu_custom_call" | custom-call | tf_op jit(solution)/shard_map/pallas_call | solution.py:462
  23.4 1.6 %copy.7 = f32[128,14,16]{0,2,1:T(8,128)} copy(f32[128,14,16]{0,2,1:T(8,128)} %bitcast.7) | data formatting | bytes 229376
